TPU v7x, 32 devices: a whole 2x2x4 slice. The times are simulated.
32 devices in a mesh: row: 8 (over z, core), col: 4 (over y, x).
Axes of the slice: x: 2, y: 2, z: 4, core: 2. Of those that a mesh axis runs over, the one named last changes fastest.
Arguments:
- psi: bfloat16 [1024, 4096], P(('row', 'col')), may hold values from -6 to 6
- hpsi: bfloat16 [1024, 4096], P(('row', 'col')), may hold values from -0.1875 to 0.1875
- eigvec: bfloat16 [4, 8, 128, 8, 4, 128], P(None, 'row', None, None, 'col'), may hold values from -0.09375 to 0.09375
Outputs:
- correlation_tiles: float32 [4, 8, 128, 8, 4, 128], P(None, 'row', None, None, 'col')
- updated_tiles: float32 [4, 8, 128, 8, 4, 128], P(None, 'row', None, None, 'col')
- diag_part: float32 [16], replicated
- offdiag_part: float32 [16], replicated
- rotated: bfloat16 [1024, 8, 4, 128], P('row', None, 'col')
All inputs are finite; a program needn't handle non-finite values.
Results may differ from a plain program's by a relative error of at most 0.001.
Values may be sent and summed in bfloat16 or wider, within the bound.
A program may use at most 128 MiB of HBM per device.

v0:
```python
import jax
import jax.numpy as jnp
from jax import lax
from jax.sharding import PartitionSpec as P

PB = 16


def broadcast(array, axis, root):
    mine = lax.axis_index(axis) == root
    return lax.psum(jnp.where(mine, array, jnp.zeros_like(array)), axis)


def inner(left, right):
    return lax.dot_general(
        left, right, (((0,), (0,)), ((), ())), preferred_element_type=jnp.float32
    )


def on_device(psi, hpsi, eigvec):
    highest = lax.Precision.HIGHEST
    g_rows = psi.shape[0]
    bands = psi.shape[1]
    row_tiles = eigvec.shape[0]
    tile_size = eigvec.shape[2]
    col_tiles = eigvec.shape[3]
    row_count = lax.axis_size("row")
    col_count = lax.axis_size("col")
    row_id = lax.axis_index("row")
    col_id = lax.axis_index("col")
    gvecs = g_rows * row_count * col_count
    row_width = row_tiles * tile_size
    col_width = col_tiles * tile_size
    lifted = (
        psi.reshape(1, g_rows, row_tiles, row_count, tile_size),
        hpsi.reshape(1, g_rows, row_tiles, row_count, tile_size),
    )
    swapped = (
        lax.all_to_all(lifted[0], "row", split_axis=3, concat_axis=0, tiled=True),
        lax.all_to_all(lifted[1], "row", split_axis=3, concat_axis=0, tiled=True),
    )
    joined = (
        lax.all_gather(swapped[0], "col", axis=1, tiled=True),
        lax.all_gather(swapped[1], "col", axis=1, tiled=True),
    )
    psi_rows = joined[0].reshape(gvecs, row_width)
    hpsi_rows = joined[1].reshape(gvecs, row_width)
    lowered = (
        psi.reshape(g_rows, col_tiles, col_count, tile_size),
        hpsi.reshape(g_rows, col_tiles, col_count, tile_size),
    )
    moved = (
        lax.all_to_all(lowered[0], "col", split_axis=2, concat_axis=0, tiled=True),
        lax.all_to_all(lowered[1], "col", split_axis=2, concat_axis=0, tiled=True),
    )
    stacked = (
        lax.all_gather(moved[0], "row", axis=0, tiled=True),
        lax.all_gather(moved[1], "row", axis=0, tiled=True),
    )
    psi_cols = stacked[0].reshape(gvecs, col_width)
    hpsi_cols = stacked[1].reshape(gvecs, col_width)
    reduced = 0.5 * (inner(psi_rows, hpsi_cols) + inner(hpsi_rows, psi_cols))
    correlation = inner(psi_rows, psi_cols) / float(gvecs)
    blocks = reduced.reshape(row_tiles, tile_size, col_tiles, tile_size)
    leading = blocks[:, :, 0, :PB]
    shared = broadcast(leading, "col", 0)
    panel = lax.all_gather(
        shared.reshape(row_tiles, 1, tile_size, PB), "row", axis=1, tiled=True
    ).reshape(bands, PB)

    def product(vector):
        local_vec = lax.dynamic_index_in_dim(
            vector.reshape(col_tiles, col_count, tile_size), col_id, 1, keepdims=False
        )
        partial_sum = jnp.einsum("atbs,bs->at", blocks, local_vec, precision=highest)
        summed = lax.psum(partial_sum, "col")
        result = lax.all_gather(
            summed.reshape(row_tiles, 1, tile_size), "row", axis=1, tiled=True
        ).reshape(bands)
        return result

    positions = jnp.arange(bands)
    slots = jnp.arange(PB)

    def reflect(step, carry):
        vecs, images, diagonal, offdiag = carry
        column = lax.dynamic_index_in_dim(panel, step, 1, keepdims=False)
        head_v = lax.dynamic_index_in_dim(vecs, step, 0, keepdims=False)
        head_w = lax.dynamic_index_in_dim(images, step, 0, keepdims=False)
        column = (
            column
            - jnp.dot(vecs, head_w, precision=highest)
            - jnp.dot(images, head_v, precision=highest)
        )
        pivot = lax.dynamic_index_in_dim(column, step + 1, 0, keepdims=False)
        below = positions > step + 1
        tail = jnp.sum(jnp.where(below, column * column, 0.0))
        length = jnp.sqrt(pivot * pivot + tail)
        beta = jnp.where(pivot >= 0.0, -length, length)
        tau = (beta - pivot) / beta
        vector = jnp.where(
            positions == step + 1, 1.0, jnp.where(below, column / (pivot - beta), 0.0)
        )
        image = product(vector)
        image = image - jnp.dot(vecs, jnp.dot(vector, images, precision=highest), precision=highest)
        image = image - jnp.dot(images, jnp.dot(vector, vecs, precision=highest), precision=highest)
        image = tau * image
        image = image - 0.5 * tau * jnp.dot(image, vector, precision=highest) * vector
        pick = slots == step
        vecs = jnp.where(pick[None, :], vector[:, None], vecs)
        images = jnp.where(pick[None, :], image[:, None], images)
        diagonal = jnp.where(
            pick, lax.dynamic_index_in_dim(column, step, 0, keepdims=False), diagonal
        )
        offdiag = jnp.where(pick, beta, offdiag)
        return (vecs, images, diagonal, offdiag)

    start_state = (
        jnp.zeros((bands, PB), jnp.float32),
        jnp.zeros((bands, PB), jnp.float32),
        jnp.zeros((PB,), jnp.float32),
        jnp.zeros((PB,), jnp.float32),
    )
    vecs, images, diagonal, offdiag = lax.fori_loop(0, PB, reflect, start_state)

    def rows_of(matrix):
        return lax.dynamic_index_in_dim(
            matrix.reshape(row_tiles, row_count, tile_size, PB), row_id, 1, keepdims=False
        ).reshape(row_width, PB)

    def cols_of(matrix):
        return lax.dynamic_index_in_dim(
            matrix.reshape(col_tiles, col_count, tile_size, PB), col_id, 1, keepdims=False
        ).reshape(col_width, PB)

    updated = (
        reduced
        - jnp.dot(rows_of(vecs), cols_of(images).T, precision=highest)
        - jnp.dot(rows_of(images), cols_of(vecs).T, precision=highest)
    )
    flat = eigvec.reshape(row_width, col_width)
    rotated = lax.psum_scatter(
        jnp.dot(psi_rows, flat, preferred_element_type=jnp.float32),
        "row",
        scatter_dimension=0,
        tiled=True,
    )
    tile_shape = (row_tiles, 1, tile_size, col_tiles, 1, tile_size)
    return (
        correlation.reshape(tile_shape),
        updated.reshape(tile_shape),
        diagonal,
        offdiag,
        rotated.astype(jnp.bfloat16).reshape(rotated.shape[0], col_tiles, 1, tile_size),
    )


def solution(mesh):
    return jax.shard_map(
        on_device,
        mesh=mesh,
        in_specs=(
            P(("row", "col"), None),
            P(("row", "col"), None),
            P(None, "row", None, None, "col", None),
        ),
        out_specs=(
            P(None, "row", None, None, "col", None),
            P(None, "row", None, None, "col", None),
            P(),
            P(),
            P("row", None, "col", None),
        ),
        check_vma=False,
    )
```

profile of v0, /device:TPU:0, one launch (start us, length us, event | category | flops | bytes accessed | tf_op | source)
XLA Modules:
  0.0 1025.6 jit_solution(13793135316026155486)
XLA Ops:
  8.4 15.9 %all_to_all.72 = bf16[1,32,4,8,128]{4,1,2,0,3:T(8,128)(2,1)S(1)} all-to-all(bf16[1,32,4,8,128]{4,1,2,0,3:T(8,128)(2,1)S(1)} %copy.46), channel_id=1, replica_groups=mesh['row'=8,'col'=4] {'row'}, dimensions={3} | all-to-all | bytes 524288 | tf_op jit(solution)/shard_map/all_to_all | solution.py:39
  25.4 12.1 %all_to_all.73 = bf16[1,32,4,8,128]{4,1,2,0,3:T(8,128)(2,1)S(1)} all-to-all(bf16[1,32,4,8,128]{4,1,2,0,3:T(8,128)(2,1)S(1)} %copy.55), channel_id=1, replica_groups=mesh['row'=8,'col'=4] {'row'}, dimensions={3} | all-to-all | bytes 524288 | tf_op jit(solution)/shard_map/all_to_all | solution.py:40
  38.6 11.8 %all_to_all.74 = bf16[32,8,4,128]{3,1,0,2:T(8,128)(2,1)} all-to-all(bf16[32,8,4,128]{3,1,0,2:T(8,128)(2,1)S(1)} %copy.52), channel_id=1, replica_groups=mesh['row'=8,'col'=4] {'col'}, dimensions={2} | all-to-all | bytes 524288 | tf_op jit(solution)/shard_map/all_to_all | solution.py:54
  65.2 15.7 %all-gather.13.cloned.1.call-done = bf16[8,1,128,4,1,128]{5,0,4,3,1,2:T(8,128)(2,1)} async-done(((bf16[8,1,32,4,1,128]{5,0,4,3,1,2:T(8,128)(2,1)}), bf16[8,1,128,4,1,128]{5,0,4,3,1,2:T(8,128)(2,1)}) %all-gather.13.cloned.1.call-update) | async-done | bytes 1048592 | tf_op jit(solution)/shard_map/all_gather | solution.py:44
  83.8 27.9 %all-gather.9.cloned.1.call-done = bf16[1024,8,1,128]{3,1,2,0:T(8,128)(2,1)} async-done(((bf16[128,8,1,128]{3,1,2,0:T(8,128)(2,1)}), bf16[1024,8,1,128]{3,1,2,0:T(8,128)(2,1)}) %all-gather.9.cloned.1.call-update) | async-done | bytes 2097168 | tf_op jit(solution)/shard_map/all_gather | solution.py:58
  117.6 24.2 %all-gather.7.cloned.1.call-done = bf16[1024,8,1,128]{3,1,2,0:T(8,128)(2,1)} async-done(((bf16[128,8,1,128]{3,1,2,0:T(8,128)(2,1)}), bf16[1024,8,1,128]{3,1,2,0:T(8,128)(2,1)}) %all-gather.7.cloned.1.call-update) | async-done | bytes 2097168 | tf_op jit(solution)/shard_map/all_gather | solution.py:57
  152.8 16.3 %psum.21 = f32[4,1,128,16]{2,3,0,1:T(8,128)S(1)} all-reduce(f32[4,1,128,16]{2,3,0,1:T(8,128)S(1)} %select_bitcast_fusion), channel_id=1, replica_groups=mesh['row'=8,'col'=4] {'col'}, use_global_device_ids=true, to_apply=%region_0.1 | all-reduce | flops 8192 | bytes 65536 | tf_op jit(solution)/shard_map/psum | solution.py:11
  169.1 15.8 %all_gather.29 = f32[4,8,128,16]{2,3,0,1:T(8,128)S(1)} all-gather(f32[4,1,128,16]{2,3,0,1:T(8,128)S(1)} %psum.21), channel_id=1, replica_groups=mesh['row'=8,'col'=4] {'row'}, dimensions={1}, use_global_device_ids=true | all-gather | bytes 294912 | tf_op jit(solution)/shard_map/all_gather | solution.py:67
  185.2 819.2 %while.23 = (s32[]{:T(128)}, f32[4096,16]{1,0:T(8,128)}, f32[4096,16]{1,0:T(8,128)}, f32[16]{0:T(128)S(1)}, f32[16]{0:T(128)S(1)}, /*index=5*/f32[4096,16]{0,1:T...) while((s32[]{:T(128)}, f32[4096,16]{1,0:T(8,128)}, ...), condition=%wide.region_4.5_spmd.clone.clone, body=%wide.region_1.4_spmd.clone.clone.sunk | while | flops 11387518 | bytes 10909649 | solution.py:124
  210.5 12.8 %all_gather.33 = f32[4,8,128]{2,0,1:T(4,128)S(1)} all-gather(f32[4,1,128]{2,0,1:T(4,128)S(1)} %psum.25), channel_id=1, replica_groups=mesh['row'=8,'col'=4] {'row'}, dimensions={1}, use_global_device_ids=true | all-gather | bytes 18432 | tf_op jit(solution)/shard_map/while/body/eval_jaxpr/all_gather | solution.py:77
  253.1 9.1 psum.25
  262.3 12.8 %all_gather.33 = f32[4,8,128]{2,0,1:T(4,128)S(1)} all-gather(f32[4,1,128]{2,0,1:T(4,128)S(1)} %psum.25), channel_id=1, replica_groups=mesh['row'=8,'col'=4] {'row'}, dimensions={1}, use_global_device_ids=true | all-gather | bytes 18432 | tf_op jit(solution)/shard_map/while/body/eval_jaxpr/all_gather | solution.py:77
  312.8 12.8 %all_gather.33 = f32[4,8,128]{2,0,1:T(4,128)S(1)} all-gather(f32[4,1,128]{2,0,1:T(4,128)S(1)} %psum.25), channel_id=1, replica_groups=mesh['row'=8,'col'=4] {'row'}, dimensions={1}, use_global_device_ids=true | all-gather | bytes 18432 | tf_op jit(solution)/shard_map/while/body/eval_jaxpr/all_gather | solution.py:77
  355.4 9.9 psum.25
  365.3 12.8 %all_gather.33 = f32[4,8,128]{2,0,1:T(4,128)S(1)} all-gather(f32[4,1,128]{2,0,1:T(4,128)S(1)} %psum.25), channel_id=1, replica_groups=mesh['row'=8,'col'=4] {'row'}, dimensions={1}, use_global_device_ids=true | all-gather | bytes 18432 | tf_op jit(solution)/shard_map/while/body/eval_jaxpr/all_gather | solution.py:77
  415.8 12.8 %all_gather.33 = f32[4,8,128]{2,0,1:T(4,128)S(1)} all-gather(f32[4,1,128]{2,0,1:T(4,128)S(1)} %psum.25), channel_id=1, replica_groups=mesh['row'=8,'col'=4] {'row'}, dimensions={1}, use_global_device_ids=true | all-gather | bytes 18432 | tf_op jit(solution)/shard_map/while/body/eval_jaxpr/all_gather | solution.py:77
  458.5 9.1 psum.25
  467.6 12.8 %all_gather.33 = f32[4,8,128]{2,0,1:T(4,128)S(1)} all-gather(f32[4,1,128]{2,0,1:T(4,128)S(1)} %psum.25), channel_id=1, replica_groups=mesh['row'=8,'col'=4] {'row'}, dimensions={1}, use_global_device_ids=true | all-gather | bytes 18432 | tf_op jit(solution)/shard_map/while/body/eval_jaxpr/all_gather | solution.py:77
  518.1 12.8 %all_gather.33 = f32[4,8,128]{2,0,1:T(4,128)S(1)} all-gather(f32[4,1,128]{2,0,1:T(4,128)S(1)} %psum.25), channel_id=1, replica_groups=mesh['row'=8,'col'=4] {'row'}, dimensions={1}, use_global_device_ids=true | all-gather | bytes 18432 | tf_op jit(solution)/shard_map/while/body/eval_jaxpr/all_gather | solution.py:77
  560.8 9.9 psum.25
  570.6 12.8 %all_gather.33 = f32[4,8,128]{2,0,1:T(4,128)S(1)} all-gather(f32[4,1,128]{2,0,1:T(4,128)S(1)} %psum.25), channel_id=1, replica_groups=mesh['row'=8,'col'=4] {'row'}, dimensions={1}, use_global_device_ids=true | all-gather | bytes 18432 | tf_op jit(solution)/shard_map/while/body/eval_jaxpr/all_gather | solution.py:77
  621.1 12.8 %all_gather.33 = f32[4,8,128]{2,0,1:T(4,128)S(1)} all-gather(f32[4,1,128]{2,0,1:T(4,128)S(1)} %psum.25), channel_id=1, replica_groups=mesh['row'=8,'col'=4] {'row'}, dimensions={1}, use_global_device_ids=true | all-gather | bytes 18432 | tf_op jit(solution)/shard_map/while/body/eval_jaxpr/all_gather | solution.py:77
  663.8 9.1 psum.25
  672.9 12.8 %all_gather.33 = f32[4,8,128]{2,0,1:T(4,128)S(1)} all-gather(f32[4,1,128]{2,0,1:T(4,128)S(1)} %psum.25), channel_id=1, replica_groups=mesh['row'=8,'col'=4] {'row'}, dimensions={1}, use_global_device_ids=true | all-gather | bytes 18432 | tf_op jit(solution)/shard_map/while/body/eval_jaxpr/all_gather | solution.py:77
  723.4 12.8 %all_gather.33 = f32[4,8,128]{2,0,1:T(4,128)S(1)} all-gather(f32[4,1,128]{2,0,1:T(4,128)S(1)} %psum.25), channel_id=1, replica_groups=mesh['row'=8,'col'=4] {'row'}, dimensions={1}, use_global_device_ids=true | all-gather | bytes 18432 | tf_op jit(solution)/shard_map/while/body/eval_jaxpr/all_gather | solution.py:77
  766.1 9.9 psum.25
  776.0 12.8 %all_gather.33 = f32[4,8,128]{2,0,1:T(4,128)S(1)} all-gather(f32[4,1,128]{2,0,1:T(4,128)S(1)} %psum.25), channel_id=1, replica_groups=mesh['row'=8,'col'=4] {'row'}, dimensions={1}, use_global_device_ids=true | all-gather | bytes 18432 | tf_op jit(solution)/shard_map/while/body/eval_jaxpr/all_gather | solution.py:77
  826.5 12.8 %all_gather.33 = f32[4,8,128]{2,0,1:T(4,128)S(1)} all-gather(f32[4,1,128]{2,0,1:T(4,128)S(1)} %psum.25), channel_id=1, replica_groups=mesh['row'=8,'col'=4] {'row'}, dimensions={1}, use_global_device_ids=true | all-gather | bytes 18432 | tf_op jit(solution)/shard_map/while/body/eval_jaxpr/all_gather | solution.py:77
  878.3 12.8 %all_gather.33 = f32[4,8,128]{2,0,1:T(4,128)S(1)} all-gather(f32[4,1,128]{2,0,1:T(4,128)S(1)} %psum.25), channel_id=1, replica_groups=mesh['row'=8,'col'=4] {'row'}, dimensions={1}, use_global_device_ids=true | all-gather | bytes 18432 | tf_op jit(solution)/shard_map/while/body/eval_jaxpr/all_gather | solution.py:77
  928.8 12.8 %all_gather.33 = f32[4,8,128]{2,0,1:T(4,128)S(1)} all-gather(f32[4,1,128]{2,0,1:T(4,128)S(1)} %psum.25), channel_id=1, replica_groups=mesh['row'=8,'col'=4] {'row'}, dimensions={1}, use_global_device_ids=true | all-gather | bytes 18432 | tf_op jit(solution)/shard_map/while/body/eval_jaxpr/all_gather | solution.py:77
  971.5 9.9 psum.25
  981.3 12.8 %all_gather.33 = f32[4,8,128]{2,0,1:T(4,128)S(1)} all-gather(f32[4,1,128]{2,0,1:T(4,128)S(1)} %psum.25), channel_id=1, replica_groups=mesh['row'=8,'col'=4] {'row'}, dimensions={1}, use_global_device_ids=true | all-gather | bytes 18432 | tf_op jit(solution)/shard_map/while/body/eval_jaxpr/all_gather | solution.py:77
  (394 shorter events, 523.9 us)
Async XLA Ops:
  7.2 18.0 %copy-start.4 = (bf16[32,4096]{1,0:T(8,128)(2,1)S(1)}, bf16[32,4096]{1,0:T(8,128)(2,1)}, u32[]{:S(2)}) copy-start(bf16[32,4096]{1,0:T(8,128)(2,1)} %param.6) | copy-start | bytes 786436
  7.2 52.5 %all-gather.11.cloned.1.call-start = ((), (), s32[]{:S(2)}) async-start(), calls=%async_computation.8 | async-start | bytes 1310720 | tf_op jit(solution)/shard_map/all_gather | solution.py:43
  25.1 55.8 %all-gather.13.cloned.1.call-start = ((), (), s32[]{:S(2)}) async-start(), calls=%async_computation.9 | async-start | bytes 1310720 | tf_op jit(solution)/shard_map/all_gather | solution.py:44
  25.2 25.4 %copy-start.5 = (bf16[32,4096]{1,0:T(8,128)(2,1)S(1)}, bf16[32,4096]{1,0:T(8,128)(2,1)}, u32[]{:S(2)}) copy-start(bf16[32,4096]{1,0:T(8,128)(2,1)} %param.5) | copy-start | bytes 786436
  38.4 73.3 %all-gather.9.cloned.1.call-start = ((), (), s32[]{:S(2)}) async-start(), calls=%async_computation.6 | async-start | bytes 2359296 | tf_op jit(solution)/shard_map/all_gather | solution.py:58
  50.5 11.5 %copy-start.8 = (bf16[4,1,128,8,1,128]{5,3,4,2,1,0:T(8,128)(2,1)S(1)}, bf16[4,1,128,8,1,128]{5,3,4,2,1,0:T(8,128)(2,1)}, u32[]{:S(2)}) copy-start(bf16[4,1,128,8,1,128]{5,3,4,2,1,0:T(8,128)(2,1)} %param.7) | copy-start | bytes 3145732
  50.5 91.2 %all-gather.7.cloned.1.call-start = ((), (), s32[]{:S(2)}) async-start(), calls=%async_computation.5 | async-start | bytes 2359296 | tf_op jit(solution)/shard_map/all_gather | solution.py:57
  59.6 957.6 %reduce-scatter.2.cloned.1.call-start = ((), (), s32[]{:S(2)}) async-start(), calls=%async_computation.7 | async-start | bytes 4718592 | tf_op jit(solution)/shard_map/reduce_scatter | solution.py:142
  145.0 4.0 copy-start.3
  149.0 2.0 copy-start.1
  185.5 3.6 copy-start
  236.1 3.6 copy-start
  287.9 3.6 copy-start
  338.4 3.6 copy-start
  390.9 3.6 copy-start
  441.4 3.6 copy-start
  493.2 3.6 copy-start
  543.7 3.6 copy-start
  596.2 3.6 copy-start
  646.7 3.6 copy-start
  698.5 3.6 copy-start
  749.0 3.6 copy-start
  801.6 3.6 copy-start
  852.1 3.6 copy-start
  903.9 3.6 copy-start
  954.4 3.6 copy-start
  1004.4 2.9 copy-start.6
  1004.4 2.9 copy-start.7
  1010.1 3.3 copy-start.2
Sparse Core Ops, SparseCore 0:
  25.2 27.5 all-gather.10
  55.3 25.5 all-gather.12
  82.5 29.1 all-gather.8
  113.2 28.5 all-gather.6
  143.9 51.4 reduce-scatter.1
where the time goes:
time: 1030 us
  blocking collectives  423 us (41%)
  matrix products  275 us (27%)
  other arithmetic  131 us (13%)
  loops' own time  77 us (7%)
  waiting for transfers between devices  67.9 us (7%)
  local copies, waits for them, and re-layouts  36.9 us (4%)
  between operations  14.1 us (1%)
    all_gather x16, blocking collectives, product(): lax.all_gather(summed.reshape(row_tiles, 1, tile_size), 'row', axis=1, ti...  204 us
    psum x16, blocking collectives, product(): summed = lax.psum(partial_sum, 'col')  139 us
    another operation x1, loops' own time, on_device(): vecs, images, diagonal, offdiag = lax.fori_loop(0, PB, reflect, start_state)  77 us
    select_n x16, other arithmetic, reflect(): images = jnp.where(pick[None, :], image[:, None], images)  61.2 us
    while x16, matrix products  56.5 us
    dot_general x16, matrix products, reflect(): jnp.dot(images, jnp.dot(vector, vecs, precision=highest), precision=highest)  54 us
    dot_general x16, matrix products, reflect(): jnp.dot(vector, images, precision=highest)  43.2 us
    while x16, other arithmetic  37.8 us
  transfers between devices with their start and end apart: 5, of which 3 were waited for; matrix products, arithmetic and copies ran while one was open for 43% of the time, Pallas kernels for 0%

commit v1 on v0

v1 whole, which is shorter than its diff:
```python
import functools

import jax
import jax.numpy as jnp
from jax import lax
from jax.experimental import pallas as pl
from jax.experimental.pallas import tpu as pltpu
from jax.sharding import PartitionSpec as P

PB = 16


def inner(left, right):
    return lax.dot_general(
        left, right, (((0,), (0,)), ((), ())), preferred_element_type=jnp.float32
    )


def total(array):
    return jnp.sum(array, axis=(0, 1), keepdims=True)


def panel_kernel(
    sizes, block, lead, vecs, images, diagonal, offdiag,
    panel, places, vector_now, folded, part, piece, gathered, full,
    lead_part, lead_piece, lead_all, col_send, col_recv, row_send, row_recv,
):
    row_count, col_count, row_tiles, col_tiles, tile = sizes
    row_id = lax.axis_index("row")
    col_id = lax.axis_index("col")

    def col_peer(distance):
        return (row_id, lax.rem(col_id + distance, col_count))

    def row_peer(distance):
        return (lax.rem(row_id + distance, row_count), col_id)

    barrier = pltpu.get_barrier_semaphore()
    for distance in range(1, col_count):
        pl.semaphore_signal(
            barrier, inc=1, device_id=col_peer(distance), device_id_type=pl.DeviceIdType.MESH
        )
    for distance in range(1, row_count):
        pl.semaphore_signal(
            barrier, inc=1, device_id=row_peer(distance), device_id_type=pl.DeviceIdType.MESH
        )
    pl.semaphore_wait(barrier, row_count + col_count - 2)

    def col_copies(source, target, slot):
        return [
            pltpu.make_async_remote_copy(
                src_ref=source,
                dst_ref=target,
                send_sem=col_send.at[slot, distance],
                recv_sem=col_recv.at[slot, distance],
                device_id=col_peer(distance),
                device_id_type=pl.DeviceIdType.MESH,
            )
            for distance in range(1, col_count)
        ]

    def row_copies(source, target, slot):
        return [
            pltpu.make_async_remote_copy(
                src_ref=source,
                dst_ref=target,
                send_sem=row_send.at[slot, distance],
                recv_sem=row_recv.at[slot, distance],
                device_id=row_peer(distance),
                device_id_type=pl.DeviceIdType.MESH,
            )
            for distance in range(1, row_count)
        ]

    copies = col_copies(lead, lead_part.at[col_id], 2)
    for copy in copies:
        copy.start()
    lead_part[pl.ds(col_id, 1)] = lead[...][None]
    vecs[...] = jnp.zeros_like(vecs)
    images[...] = jnp.zeros_like(images)
    diagonal[...] = jnp.zeros_like(diagonal)
    offdiag[...] = jnp.zeros_like(offdiag)
    lanes = lax.broadcasted_iota(jnp.int32, (row_tiles, tile), 1)
    tiles = lax.broadcasted_iota(jnp.int32, (row_tiles, tile), 0)
    for owner in range(row_count):
        places[owner * row_tiles : (owner + 1) * row_tiles, :] = (
            tiles * row_count + owner
        ) * tile + lanes
    for copy in copies:
        copy.wait()
    summed = lead_part[0]
    for source in range(1, col_count):
        summed = summed + lead_part[source]
    lead_piece[...] = summed
    copies = row_copies(lead_piece, lead_all.at[row_id], 2)
    for copy in copies:
        copy.start()
    lead_all[pl.ds(row_id, 1)] = summed[None]
    for copy in copies:
        copy.wait()
    for owner in range(row_count):
        panel[:, owner * row_tiles : (owner + 1) * row_tiles, :] = lead_all[owner]

    pos = places[...]
    lane = lax.broadcasted_iota(jnp.int32, (1, tile), 1)
    lane3 = lax.broadcasted_iota(jnp.int32, (PB, 1, tile), 2)
    chunk = 64
    rows = row_tiles * tile

    @pl.loop(0, PB)
    def _(step):
        slot = lax.rem(step, 2)
        head_v = jnp.sum(jnp.where(lane3 == step, vecs[:, 0:1, :], 0.0), axis=2, keepdims=True)
        head_w = jnp.sum(jnp.where(lane3 == step, images[:, 0:1, :], 0.0), axis=2, keepdims=True)
        column = panel[step]
        for k in range(PB - 1):
            column = column - vecs[k] * head_w[k] - images[k] * head_v[k]
        below = pos > step + 1
        pivot = total(jnp.where(pos == step + 1, column, 0.0))
        here = total(jnp.where(pos == step, column, 0.0))
        tail = total(jnp.where(below, column * column, 0.0))
        length = jnp.sqrt(pivot * pivot + tail)
        beta = jnp.where(pivot >= 0.0, -length, length)
        tau = (beta - pivot) / beta
        vector = jnp.where(
            pos == step + 1, 1.0, jnp.where(below, column / (pivot - beta), 0.0)
        )
        vector_now[...] = vector
        local = []
        for g in range(col_tiles):
            b = col_id + col_count * g
            local.append(
                vector_now[pl.ds(lax.rem(b, row_count) * row_tiles + lax.div(b, row_count), 1), :]
            )
        for start in range(0, rows, chunk):
            acc = block[start : start + chunk, 0:tile] * local[0]
            for g in range(1, col_tiles):
                acc = acc + block[start : start + chunk, g * tile : (g + 1) * tile] * local[g]
            folded[start : start + chunk, :] = acc
        sums = lax.dot_general(
            jnp.ones((8, tile), jnp.float32),
            folded[...],
            (((1,), (1,)), ((), ())),
            precision=lax.Precision.HIGHEST,
            preferred_element_type=jnp.float32,
        )
        for t in range(row_tiles):
            part[step, col_id, t : t + 1, :] = sums[0:1, t * tile : (t + 1) * tile]
        sent = col_copies(part.at[step, col_id], part.at[step, col_id], slot)
        for copy in sent:
            copy.start()
        onto_w = [total(images[k] * vector) for k in range(PB - 1)]
        onto_v = [total(vecs[k] * vector) for k in range(PB - 1)]
        fix = vecs[0] * onto_w[0] + images[0] * onto_v[0]
        for k in range(1, PB - 1):
            fix = fix + vecs[k] * onto_w[k] + images[k] * onto_v[k]
        vecs[pl.ds(step, 1)] = vector[None]
        diagonal[...] = jnp.where(lane == step, here, diagonal[...])
        offdiag[...] = jnp.where(lane == step, beta, offdiag[...])
        for copy in sent:
            copy.wait()
        image = part[step, 0]
        for source in range(1, col_count):
            image = image + part[step, source]
        gathered[step, row_id] = image
        sent = row_copies(gathered.at[step, row_id], gathered.at[step, row_id], slot)
        for copy in sent:
            copy.start()
        for copy in sent:
            copy.wait()
        for owner in range(row_count):
            full[owner * row_tiles : (owner + 1) * row_tiles, :] = gathered[step, owner]
        image = tau * (full[...] - fix)
        image = image - 0.5 * tau * total(image * vector) * vector
        images[pl.ds(step, 1)] = image[None]


def reduce_panel(block, lead, sizes):
    row_count, col_count, row_tiles, col_tiles, tile = sizes
    all_tiles = row_count * row_tiles
    f32 = jnp.float32
    whole = pl.BlockSpec(memory_space=pltpu.VMEM)
    return pl.pallas_call(
        functools.partial(panel_kernel, sizes),
        out_shape=(
            jax.ShapeDtypeStruct((PB, all_tiles, tile), f32),
            jax.ShapeDtypeStruct((PB, all_tiles, tile), f32),
            jax.ShapeDtypeStruct((1, tile), f32),
            jax.ShapeDtypeStruct((1, tile), f32),
        ),
        in_specs=[whole, whole],
        out_specs=(whole, whole, whole, whole),
        scratch_shapes=[
            pltpu.VMEM((PB, all_tiles, tile), f32),
            pltpu.VMEM((all_tiles, tile), jnp.int32),
            pltpu.VMEM((all_tiles, tile), f32),
            pltpu.VMEM((row_tiles * tile, tile), f32),
            pltpu.VMEM((PB, col_count, row_tiles, tile), f32),
            pltpu.VMEM((row_tiles, tile), f32),
            pltpu.VMEM((PB, row_count, row_tiles, tile), f32),
            pltpu.VMEM((all_tiles, tile), f32),
            pltpu.VMEM((col_count, PB, row_tiles, tile), f32),
            pltpu.VMEM((PB, row_tiles, tile), f32),
            pltpu.VMEM((row_count, PB, row_tiles, tile), f32),
            pltpu.SemaphoreType.DMA((3, col_count)),
            pltpu.SemaphoreType.DMA((3, col_count)),
            pltpu.SemaphoreType.DMA((3, row_count)),
            pltpu.SemaphoreType.DMA((3, row_count)),
        ],
        compiler_params=pltpu.CompilerParams(
            collective_id=0, has_side_effects=True, vmem_limit_bytes=24 * 1024 * 1024
        ),
        cost_estimate=pl.CostEstimate(
            flops=400_000_000, bytes_accessed=4_000_000, transcendentals=0
        ),
        name="panel",
    )(block, lead)


def on_device(psi, hpsi, eigvec):
    highest = lax.Precision.HIGHEST
    g_rows = psi.shape[0]
    bands = psi.shape[1]
    row_tiles = eigvec.shape[0]
    tile_size = eigvec.shape[2]
    col_tiles = eigvec.shape[3]
    row_count = lax.axis_size("row")
    col_count = lax.axis_size("col")
    row_id = lax.axis_index("row")
    col_id = lax.axis_index("col")
    gvecs = g_rows * row_count * col_count
    row_width = row_tiles * tile_size
    col_width = col_tiles * tile_size
    lifted = (
        psi.reshape(1, g_rows, row_tiles, row_count, tile_size),
        hpsi.reshape(1, g_rows, row_tiles, row_count, tile_size),
    )
    swapped = (
        lax.all_to_all(lifted[0], "row", split_axis=3, concat_axis=0, tiled=True),
        lax.all_to_all(lifted[1], "row", split_axis=3, concat_axis=0, tiled=True),
    )
    joined = (
        lax.all_gather(swapped[0], "col", axis=1, tiled=True),
        lax.all_gather(swapped[1], "col", axis=1, tiled=True),
    )
    psi_rows = joined[0].reshape(gvecs, row_width)
    hpsi_rows = joined[1].reshape(gvecs, row_width)
    lowered = (
        psi.reshape(g_rows, col_tiles, col_count, tile_size),
        hpsi.reshape(g_rows, col_tiles, col_count, tile_size),
    )
    moved = (
        lax.all_to_all(lowered[0], "col", split_axis=2, concat_axis=0, tiled=True),
        lax.all_to_all(lowered[1], "col", split_axis=2, concat_axis=0, tiled=True),
    )
    stacked = (
        lax.all_gather(moved[0], "row", axis=0, tiled=True),
        lax.all_gather(moved[1], "row", axis=0, tiled=True),
    )
    psi_cols = stacked[0].reshape(gvecs, col_width)
    hpsi_cols = stacked[1].reshape(gvecs, col_width)
    reduced = 0.5 * (inner(psi_rows, hpsi_cols) + inner(hpsi_rows, psi_cols))
    correlation = inner(psi_rows, psi_cols) / float(gvecs)
    blocks = reduced.reshape(row_tiles, tile_size, col_tiles, tile_size)
    leading = blocks[:, :, 0, :PB]
    lead = jnp.where(col_id == 0, jnp.transpose(leading, (2, 0, 1)), 0.0)
    sizes = (row_count, col_count, row_tiles, col_tiles, tile_size)
    vecs, images, diagonal, offdiag = reduce_panel(reduced, lead, sizes)
    diagonal = diagonal[0, :PB]
    offdiag = offdiag[0, :PB]

    def rows_of(matrix):
        return lax.dynamic_index_in_dim(
            matrix.reshape(PB, row_count, row_tiles, tile_size), row_id, 1, keepdims=False
        ).reshape(PB, row_width)

    def cols_of(matrix):
        ordered = jnp.transpose(
            matrix.reshape(PB, row_count, row_tiles, tile_size), (0, 2, 1, 3)
        )
        return lax.dynamic_index_in_dim(
            ordered.reshape(PB, col_tiles, col_count, tile_size), col_id, 2, keepdims=False
        ).reshape(PB, col_width)

    left = jnp.concatenate([rows_of(vecs), rows_of(images)], axis=0)
    right = jnp.concatenate([cols_of(images), cols_of(vecs)], axis=0)
    updated = reduced - lax.dot_general(
        left, right, (((0,), (0,)), ((), ())), precision=highest,
        preferred_element_type=jnp.float32,
    )
    flat = eigvec.reshape(row_width, col_width)
    rotated = lax.psum_scatter(
        jnp.dot(psi_rows, flat, preferred_element_type=jnp.float32),
        "row",
        scatter_dimension=0,
        tiled=True,
    )
    tile_shape = (row_tiles, 1, tile_size, col_tiles, 1, tile_size)
    return (
        correlation.reshape(tile_shape),
        updated.reshape(tile_shape),
        diagonal,
        offdiag,
        rotated.astype(jnp.bfloat16).reshape(rotated.shape[0], col_tiles, 1, tile_size),
    )


def solution(mesh):
    return jax.shard_map(
        on_device,
        mesh=mesh,
        in_specs=(
            P(("row", "col"), None),
            P(("row", "col"), None),
            P(None, "row", None, None, "col", None),
        ),
        out_specs=(
            P(None, "row", None, None, "col", None),
            P(None, "row", None, None, "col", None),
            P(),
            P(),
            P("row", None, "col", None),
        ),
        check_vma=False,
    )
```

time: 1030 us -> 298 us (0.29)
  blocking collectives: 423 us -> 48.7 us
  matrix products: 275 us -> 9.01 us
  Pallas kernels: 0 us -> 136 us
  other arithmetic: 131 us -> 1.09 us
  loops' own time: 77 us -> 0 us
  local copies, waits for them, and re-layouts: 36.9 us -> 21.7 us
    all_gather x17 -> x0, blocking collectives: 220 us -> none  [the longest x16 204 us: product(): lax.all_gather(summed.reshape(row_tiles, 1, tile_size), 'row', axis=1, ti...]
    dot_general x98 -> x1, matrix products: 206 us -> 1.9 us  [on_device(): lax.dot_general(left, right, (((0,), (0,)), ((), ())), precision=highest,...]
    psum x17 -> x0, blocking collectives: 155 us -> none  [the longest x16 139 us: product(): summed = lax.psum(partial_sum, 'col')]
    pallas_call x0 -> x1, Pallas kernels: none -> 136 us  [reduce_panel(): pl.pallas_call(functools.partial(panel_kernel, sizes), out_shape=(jax.Sha...]
    another operation x1 -> x0, loops' own time: 77 us -> none  [on_device(): vecs, images, diagonal, offdiag = lax.fori_loop(0, PB, reflect, start_state)]
    select_n x64 -> x1, other arithmetic: 72 us -> 0.02 us  [on_device(): lead = jnp.where(col_id == 0, jnp.transpose(leading, (2, 0, 1)), 0.0)]
    while x16 -> x0, matrix products: 56.5 us -> none
    while x16 -> x0, other arithmetic: 37.8 us -> none
  transfers between devices with their start and end apart: 5 -> 5, of which waited for: 3 -> 3; matrix products, arithmetic and copies ran while one was open for 43% -> 9% of each run, Pallas kernels for 0% -> 46%
where the time goes in v1:
time: 298 us
  Pallas kernels  136 us (46%)
  waiting for transfers between devices  66.9 us (22%)
  blocking collectives  48.7 us (16%)
  local copies, waits for them, and re-layouts  21.7 us (7%)
  between operations  14.1 us (5%)
  matrix products  9.01 us (3%)
    pallas_call x1, Pallas kernels, reduce_panel(): pl.pallas_call(functools.partial(panel_kernel, sizes), out_shape=(jax.Sha...  136 us
    all_gather x1, waiting for transfers between devices, on_device(): lax.all_gather(moved[0], 'row', axis=0, tiled=True)  27.9 us
    all_gather x1, waiting for transfers between devices, on_device(): lax.all_gather(moved[1], 'row', axis=0, tiled=True)  23.7 us
    all_to_all x1, blocking collectives, on_device(): lax.all_to_all(lifted[0], 'row', split_axis=3, concat_axis=0, tiled=True)  15.9 us
    all_gather x1, waiting for transfers between devices, on_device(): lax.all_gather(swapped[1], 'col', axis=1, tiled=True)  15.2 us
    all_to_all x1, blocking collectives, on_device(): lax.all_to_all(lifted[1], 'row', split_axis=3, concat_axis=0, tiled=True)  12.1 us
    all_to_all x1, blocking collectives, on_device(): lax.all_to_all(lowered[0], 'col', split_axis=2, concat_axis=0, tiled=True)  11.8 us
    all_to_all x1, blocking collectives, on_device(): lax.all_to_all(lowered[1], 'col', split_axis=2, concat_axis=0, tiled=True)  8.92 us
  transfers between devices with their start and end apart: 5, of which 3 were waited for; matrix products, arithmetic and copies ran while one was open for 9% of the time, Pallas kernels for 46%

profile of v1, /device:TPU:0, one launch (start us, length us, event | category | flops | bytes accessed | tf_op | source)
XLA Modules:
  0.0 297.9 jit_solution(3635411684860824833)
XLA Ops:
  7.2 1.0 copy.76
  8.4 15.9 %all_to_all.72 = bf16[1,32,4,8,128]{4,1,2,0,3:T(8,128)(2,1)S(1)} all-to-all(bf16[1,32,4,8,128]{4,1,2,0,3:T(8,128)(2,1)S(1)} %copy.54), channel_id=1, replica_groups=mesh['row'=8,'col'=4] {'row'}, dimensions={3} | all-to-all | bytes 524288 | tf_op jit(solution)/shard_map/all_to_all | solution.py:239
  24.2 0.9 copy.55
  25.4 12.1 %all_to_all.73 = bf16[1,32,4,8,128]{4,1,2,0,3:T(8,128)(2,1)S(1)} all-to-all(bf16[1,32,4,8,128]{4,1,2,0,3:T(8,128)(2,1)S(1)} %copy.63), channel_id=1, replica_groups=mesh['row'=8,'col'=4] {'row'}, dimensions={3} | all-to-all | bytes 524288 | tf_op jit(solution)/shard_map/all_to_all | solution.py:240
  37.5 0.9 copy.64
  38.4 0.2 reshape.84
  38.7 11.8 %all_to_all.74 = bf16[32,8,4,128]{3,1,0,2:T(8,128)(2,1)} all-to-all(bf16[32,8,4,128]{3,1,0,2:T(8,128)(2,1)S(1)} %copy.57), channel_id=1, replica_groups=mesh['row'=8,'col'=4] {'col'}, dimensions={2} | all-to-all | bytes 524288 | tf_op jit(solution)/shard_map/all_to_all | solution.py:253
  50.6 0.2 reshape.87
  50.8 8.9 %all_to_all.75 = bf16[32,8,4,128]{3,1,0,2:T(8,128)(2,1)} all-to-all(bf16[32,8,4,128]{3,1,0,2:T(8,128)(2,1)S(1)} %copy.60), channel_id=1, replica_groups=mesh['row'=8,'col'=4] {'col'}, dimensions={2} | all-to-all | bytes 524288 | tf_op jit(solution)/shard_map/all_to_all | solution.py:254
  59.8 2.2 copy.56
  62.0 3.2 %fusion = f32[1024,1024]{1,0:T(8,128)} fusion(bf16[64,8,8,128]{3,2,1,0:T(8,128)(2,1)S(1)} %bitcast.151, bf16[64,8,8,128]{3,2,1,0:T(8,128)(2,1)S(1)} %bitcast.128), kind=kOutput, calls=%fused_computation.3 | convolution fusion | flops 1073741824 | bytes 6291456 | tf_op jit(solution)/shard_map/dot_general | solution.py:293
  65.3 15.2 %all-gather.13.cloned.1.call-done = bf16[8,1,128,4,1,128]{5,0,4,3,1,2:T(8,128)(2,1)} async-done(((bf16[8,1,32,4,1,128]{5,0,4,3,1,2:T(8,128)(2,1)}), bf16[8,1,128,4,1,128]{5,0,4,3,1,2:T(8,128)(2,1)}) %all-gather.13.cloned.1.call-update) | async-done | bytes 1048592 | tf_op jit(solution)/shard_map/all_gather | solution.py:244
  80.6 2.9 copy.65
  83.5 27.9 %all-gather.7.cloned.1.call-done = bf16[1024,8,1,128]{3,1,2,0:T(8,128)(2,1)} async-done(((bf16[128,8,1,128]{3,1,2,0:T(8,128)(2,1)}), bf16[1024,8,1,128]{3,1,2,0:T(8,128)(2,1)}) %all-gather.7.cloned.1.call-update) | async-done | bytes 2097168 | tf_op jit(solution)/shard_map/all_gather | solution.py:257
  111.3 3.2 %copy.59 = bf16[1024,8,1,128]{0,3,1,2:T(8,128)(2,1)S(1)} copy(bf16[1024,8,1,128]{3,1,2,0:T(8,128)(2,1)} %all-gather.7.cloned.1.call-done) | data formatting | bytes 4194304 | tf_op jit(solution)/shard_map/all_gather | solution.py:257
  114.6 1.3 multiply_bitcast_fusion
  115.9 1.8 copy.78
  117.7 23.7 %all-gather.9.cloned.1.call-done = bf16[1024,8,1,128]{3,1,2,0:T(8,128)(2,1)} async-done(((bf16[128,8,1,128]{3,1,2,0:T(8,128)(2,1)}), bf16[1024,8,1,128]{3,1,2,0:T(8,128)(2,1)}) %all-gather.9.cloned.1.call-update) | async-done | bytes 2097168 | tf_op jit(solution)/shard_map/all_gather | solution.py:258
  141.4 3.2 %copy.62 = bf16[1024,8,1,128]{0,3,1,2:T(8,128)(2,1)S(1)} copy(bf16[1024,8,1,128]{3,1,2,0:T(8,128)(2,1)} %all-gather.9.cloned.1.call-done) | data formatting | bytes 4194304 | tf_op jit(solution)/shard_map/all_gather | solution.py:258
  144.7 1.3 fusion.6
  145.9 0.3 copy-done.1
  146.2 0.3 copy-done.2
  146.5 1.3 add_multiply_fusion.block
  147.8 0.5 copy.81
  148.5 136.3 %panel.1 = (f32[16,32,128]{2,1,0:T(8,128)S(1)}, f32[16,32,128]{2,1,0:T(8,128)S(1)}, f32[1,128]{1,0:T(1,128)S(1)}, f32[1,128]{1,0:T(1,128)S(1)}) custom-call(f32[512,1024]{1,0:T(8,128)S(1)} %add_multiply_fusion.block, f32[16,4,128]{2,1,0:T(4,128)S(1)} %select_bitcast_fusion.lead), custom_call_target="tpu_custom_call" | custom-call | flops 400000000 | bytes 4000000 | tf_op jit(solution)/shard_map/panel/pallas_call | solution.py:183
  284.8 0.2 copy.69
  285.0 0.2 copy.67
  285.4 1.9 subtract_bitcast_fusion
  287.3 1.8 copy.86
  289.1 0.5 slice_bitcast_fusion
  289.6 1.1 convert_bitcast_fusion
  290.7 0.8 copy.88
  (38 shorter events, 1.1 us)
Async XLA Ops:
  7.2 18.0 %copy-start.4 = (bf16[32,4096]{1,0:T(8,128)(2,1)S(1)}, bf16[32,4096]{1,0:T(8,128)(2,1)}, u32[]{:S(2)}) copy-start(bf16[32,4096]{1,0:T(8,128)(2,1)} %param.4) | copy-start | bytes 786436
  7.2 52.6 %all-gather.11.cloned.1.call-start = ((), (), s32[]{:S(2)}) async-start(), calls=%async_computation.8 | async-start | bytes 1310720 | tf_op jit(solution)/shard_map/all_gather | solution.py:243
  8.3 30.2 %copy-start.3 = (bf16[32,4096]{1,0:T(8,128)(2,1)S(1)}, bf16[32,4096]{1,0:T(8,128)(2,1)}, u32[]{:S(2)}) copy-start(bf16[32,4096]{1,0:T(8,128)(2,1)} %param.3) | copy-start | bytes 786436
  25.1 55.4 %all-gather.13.cloned.1.call-start = ((), (), s32[]{:S(2)}) async-start(), calls=%async_computation.9 | async-start | bytes 1310720 | tf_op jit(solution)/shard_map/all_gather | solution.py:244
  38.4 73.0 %all-gather.7.cloned.1.call-start = ((), (), s32[]{:S(2)}) async-start(), calls=%async_computation.5 | async-start | bytes 2359296 | tf_op jit(solution)/shard_map/all_gather | solution.py:257
  50.5 11.6 %copy-start.5 = (bf16[4,1,128,8,1,128]{5,3,4,2,1,0:T(8,128)(2,1)S(1)}, bf16[4,1,128,8,1,128]{5,3,4,2,1,0:T(8,128)(2,1)}, u32[]{:S(2)}) copy-start(bf16[4,1,128,8,1,128]{5,3,4,2,1,0:T(8,128)(2,1)} %param.5) | copy-start | bytes 3145732
  50.5 90.9 %all-gather.9.cloned.1.call-start = ((), (), s32[]{:S(2)}) async-start(), calls=%async_computation.6 | async-start | bytes 2359296 | tf_op jit(solution)/shard_map/all_gather | solution.py:258
  59.7 229.8 %reduce-scatter.2.cloned.1.call-start = ((), (), s32[]{:S(2)}) async-start(), calls=%async_computation.7 | async-start | bytes 4718592 | tf_op jit(solution)/shard_map/reduce_scatter | solution.py:292
  114.6 1.3 copy-start
  144.6 1.6 copy-start.1
  144.6 1.8 copy-start.2
Sparse Core Ops, SparseCore 0:
  25.3 27.5 all-gather.10
  55.3 25.1 all-gather.12
  82.2 29.1 all-gather.6
  112.8 28.5 all-gather.8
  143.5 54.5 reduce-scatter.1

commit v2 on v1

--- a/solution.py
+++ b/solution.py
@@ -217,6 +217,154 @@
     )(block, lead)
 
 
+def spread_kernel(
+    row_count, col_count, rows_in, cols_in, row_all, col_all,
+    own_sem, a1_send, a1_recv, a2_send, a2_recv, b1_send, b1_recv,
+    right_send, right_recv, left_send, left_recv, pair_send, pair_recv,
+):
+    row_id = lax.axis_index("row")
+    col_id = lax.axis_index("col")
+    ring = row_count // 2
+    half = ring // 2
+
+    def row_at(shift):
+        return lax.rem(row_id + shift + row_count, row_count)
+
+    def col_peer(distance):
+        return (row_id, lax.rem(col_id + distance, col_count))
+
+    barrier = pltpu.get_barrier_semaphore()
+    for distance in range(1, col_count):
+        pl.semaphore_signal(
+            barrier, inc=1, device_id=col_peer(distance), device_id_type=pl.DeviceIdType.MESH
+        )
+    for distance in range(1, row_count):
+        pl.semaphore_signal(
+            barrier, inc=1, device_id=(row_at(distance), col_id),
+            device_id_type=pl.DeviceIdType.MESH,
+        )
+    pl.semaphore_wait(barrier, row_count + col_count - 2)
+
+    def remote(source, target, send, recv, device):
+        return pltpu.make_async_remote_copy(
+            src_ref=source, dst_ref=target, send_sem=send, recv_sem=recv,
+            device_id=device, device_id_type=pl.DeviceIdType.MESH,
+        )
+
+    own = [
+        pltpu.make_async_copy(cols_in.at[col_id], col_all.at[:, row_id, col_id], own_sem.at[0]),
+        pltpu.make_async_copy(rows_in.at[row_id], row_all.at[:, row_id, col_id], own_sem.at[1]),
+    ]
+    b1 = []
+    for d in range(1, col_count):
+        peer = col_peer(d)
+        b1.append(remote(
+            cols_in.at[peer[1]], col_all.at[:, row_id, col_id], b1_send.at[d], b1_recv.at[d], peer
+        ))
+    a1 = []
+    for d in range(1, row_count):
+        peer = row_at(d)
+        a1.append(remote(
+            rows_in.at[peer], row_all.at[:, row_id, col_id], a1_send.at[d], a1_recv.at[d],
+            (peer, col_id),
+        ))
+    for copy in b1 + own + a1:
+        copy.start()
+    own[0].wait()
+    for copy in b1:
+        copy.wait()
+
+    def forward(step, origin, shift, final_part, send, recv):
+        place = col_all.at[:, origin] if step < half else col_all.at[final_part, origin]
+        return remote(place, place, send.at[step], recv.at[step], (row_at(shift), col_id))
+
+    partner = row_id + 1 - 2 * lax.rem(row_id, 2)
+
+    def to_partner(index, origin):
+        place = col_all.at[:, origin]
+        return remote(place, place, pair_send.at[index], pair_recv.at[index], (partner, col_id))
+
+    right = [forward(1, row_id, 2, 0, right_send, right_recv)]
+    left = [forward(1, row_id, -2, 1, left_send, left_recv)]
+    pairs = [to_partner(0, row_id)]
+    right[0].start()
+    left[0].start()
+    pairs[0].start()
+    own[1].wait()
+    for copy in a1:
+        copy.wait()
+    a2 = []
+    for d in range(1, col_count):
+        place = row_all.at[:, :, col_id]
+        a2.append(remote(place, place, a2_send.at[d], a2_recv.at[d], col_peer(d)))
+        a2[-1].start()
+    for step in range(1, half):
+        from_left = row_at(-2 * step)
+        from_right = row_at(2 * step)
+        right[-1].wait_recv()
+        right.append(forward(step + 1, from_left, 2, 0, right_send, right_recv))
+        right[-1].start()
+        left[-1].wait_recv()
+        left.append(forward(step + 1, from_right, -2, 1, left_send, left_recv))
+        left[-1].start()
+        for index, origin in ((2 * step - 1, from_left), (2 * step, from_right)):
+            pairs.append(to_partner(index, origin))
+            pairs[-1].start()
+    right[-1].wait_recv()
+    left[-1].wait_recv()
+    pairs.append(to_partner(ring - 1, row_at(2 * half)))
+    pairs[-1].start()
+    for copy in a2:
+        copy.wait()
+    for copy in pairs:
+        copy.wait()
+    for copy in right + left:
+        copy.wait_send()
+
+
+def spread(psi, hpsi, row_count, col_count, row_tiles, col_tiles, tile):
+    g_rows = psi.shape[0]
+    both = jnp.stack([psi, hpsi])
+    rows_in = jnp.transpose(
+        both.reshape(2, g_rows, row_tiles, row_count, tile), (3, 0, 1, 2, 4)
+    ).reshape(row_count, 2, g_rows, row_tiles * tile)
+    cols_in = jnp.transpose(
+        both.reshape(2, g_rows, col_tiles, col_count, tile), (3, 0, 1, 2, 4)
+    ).reshape(col_count, 2, g_rows, col_tiles * tile)
+    whole = pl.BlockSpec(memory_space=pltpu.VMEM)
+    hbm = pl.BlockSpec(memory_space=pltpu.VMEM)
+    ring = row_count // 2
+    dma = pltpu.SemaphoreType.DMA
+    return pl.pallas_call(
+        functools.partial(spread_kernel, row_count, col_count),
+        out_shape=(
+            jax.ShapeDtypeStruct(
+                (2, row_count, col_count, g_rows, row_tiles * tile), psi.dtype
+            ),
+            jax.ShapeDtypeStruct(
+                (2, row_count, col_count, g_rows, col_tiles * tile), psi.dtype
+            ),
+        ),
+        in_specs=[whole, whole],
+        out_specs=(hbm, hbm),
+        scratch_shapes=[
+            dma((2,)),
+            dma((row_count,)), dma((row_count,)),
+            dma((col_count,)), dma((col_count,)),
+            dma((col_count,)), dma((col_count,)),
+            dma((ring,)), dma((ring,)), dma((ring,)), dma((ring,)),
+            dma((ring,)), dma((ring,)),
+        ],
+        compiler_params=pltpu.CompilerParams(
+            collective_id=1, has_side_effects=True, vmem_limit_bytes=40 * 1024 * 1024
+        ),
+        cost_estimate=pl.CostEstimate(
+            flops=100_000_000, bytes_accessed=8_000_000, transcendentals=0
+        ),
+        name="spread",
+    )(rows_in, cols_in)
+
+
 def on_device(psi, hpsi, eigvec):
     highest = lax.Precision.HIGHEST
     g_rows = psi.shape[0]
@@ -231,34 +379,13 @@
     gvecs = g_rows * row_count * col_count
     row_width = row_tiles * tile_size
     col_width = col_tiles * tile_size
-    lifted = (
-        psi.reshape(1, g_rows, row_tiles, row_count, tile_size),
-        hpsi.reshape(1, g_rows, row_tiles, row_count, tile_size),
-    )
-    swapped = (
-        lax.all_to_all(lifted[0], "row", split_axis=3, concat_axis=0, tiled=True),
-        lax.all_to_all(lifted[1], "row", split_axis=3, concat_axis=0, tiled=True),
-    )
-    joined = (
-        lax.all_gather(swapped[0], "col", axis=1, tiled=True),
-        lax.all_gather(swapped[1], "col", axis=1, tiled=True),
-    )
-    psi_rows = joined[0].reshape(gvecs, row_width)
-    hpsi_rows = joined[1].reshape(gvecs, row_width)
-    lowered = (
-        psi.reshape(g_rows, col_tiles, col_count, tile_size),
-        hpsi.reshape(g_rows, col_tiles, col_count, tile_size),
-    )
-    moved = (
-        lax.all_to_all(lowered[0], "col", split_axis=2, concat_axis=0, tiled=True),
-        lax.all_to_all(lowered[1], "col", split_axis=2, concat_axis=0, tiled=True),
-    )
-    stacked = (
-        lax.all_gather(moved[0], "row", axis=0, tiled=True),
-        lax.all_gather(moved[1], "row", axis=0, tiled=True),
-    )
-    psi_cols = stacked[0].reshape(gvecs, col_width)
-    hpsi_cols = stacked[1].reshape(gvecs, col_width)
+    row_all, col_all = spread(
+        psi, hpsi, row_count, col_count, row_tiles, col_tiles, tile_size
+    )
+    psi_rows = row_all[0].reshape(gvecs, row_width)
+    hpsi_rows = row_all[1].reshape(gvecs, row_width)
+    psi_cols = col_all[0].reshape(gvecs, col_width)
+    hpsi_cols = col_all[1].reshape(gvecs, col_width)
     reduced = 0.5 * (inner(psi_rows, hpsi_cols) + inner(hpsi_rows, psi_cols))
     correlation = inner(psi_rows, psi_cols) / float(gvecs)
     blocks = reduced.reshape(row_tiles, tile_size, col_tiles, tile_size)

time: 298 us -> 232 us (0.78)
  waiting for transfers between devices: 66.9 us -> 0.02 us
  Pallas kernels: 136 us -> 191 us
  blocking collectives: 48.7 us -> 0 us
  local copies, waits for them, and re-layouts: 21.7 us -> 13.2 us
    all_gather x4 -> x0, waiting for transfers between devices: 66.8 us -> none  [the longest x1 27.9 us: on_device(): lax.all_gather(moved[0], 'row', axis=0, tiled=True)]
    pallas_call x0 -> x1, Pallas kernels: none -> 54.6 us  [spread(): pl.pallas_call(functools.partial(spread_kernel, row_count, col_count), ou...]
    all_to_all x4 -> x0, blocking collectives: 48.7 us -> none  [the longest x1 15.9 us: on_device(): lax.all_to_all(lifted[0], 'row', split_axis=3, concat_axis=0, tiled=True)]
    all_gather x4 -> x0, local copies, waits for them, and re-layouts: 11.6 us -> none  [the longest x1 3.24 us: on_device(): lax.all_gather(moved[0], 'row', axis=0, tiled=True)]
    unnamed x23 -> x21, local copies, waits for them, and re-layouts: 6.57 us -> 9.07 us
  transfers between devices with their start and end apart: 5 -> 1, of which waited for: 3 -> 0; matrix products, arithmetic and copies ran while one was open for 9% -> 6% of each run, Pallas kernels for 46% -> 59%
where the time goes in v2:
time: 232 us
  Pallas kernels  191 us (82%)
  between operations  14.3 us (6%)
  local copies, waits for them, and re-layouts  13.2 us (6%)
  matrix products  11.7 us (5%)
    pallas_call x1, Pallas kernels, reduce_panel(): pl.pallas_call(functools.partial(panel_kernel, sizes), out_shape=(jax.Sha...  137 us
    pallas_call x1, Pallas kernels, spread(): pl.pallas_call(functools.partial(spread_kernel, row_count, col_count), ou...  54.6 us
    unnamed x21, local copies, waits for them, and re-layouts  9.07 us
    dot_general x3, matrix products, inner(): lax.dot_general(left, right, (((0,), (0,)), ((), ())), preferred_element_...  6.62 us
  transfers between devices with their start and end apart: 1, of which 0 were waited for; matrix products, arithmetic and copies ran while one was open for 6% of the time, Pallas kernels for 59%

profile of v2, /device:TPU:0, one launch (start us, length us, event | category | flops | bytes accessed | tf_op | source)
XLA Modules:
  0.0 232.0 jit_solution(17439124830669425485)
XLA Ops:
  7.2 0.0 copy-start.3
  7.2 0.0 reduce-scatter.2.cloned.1.call-start
  7.2 1.2 stack.19
  8.4 1.0 copy.44
  9.4 0.1 copy.27
  9.5 1.1 stack.18
  10.7 0.1 copy.26
  10.8 0.3 maximum_bitcast_fusion
  11.1 0.2 reshape.88.rows_in
  11.4 0.1 maximum_bitcast_fusion.1
  11.5 0.2 reshape.89.cols_in
  11.7 54.6 %spread.1 = (bf16[2,8,4,32,512]{4,3,2,1,0:T(8,128)(2,1)S(1)}, bf16[2,8,4,32,1024]{4,3,2,1,0:T(8,128)(2,1)S(1)}) custom-call(bf16[8,2,32,512]{3,2,1,0:T(8,128)(2,1)S(1)} %reshape.88.rows_in, bf16[4,2,32,1024]{3,2,1,0:T(8,128)(2,1)S(1)} %reshape.89.cols_in), custom_call_target="tpu_custom_call" | custom-call | flops 100000000 | bytes 8000000 | tf_op jit(solution)/shard_map/spread/pallas_call | solution.py:338
  66.3 1.9 copy-done.1
  68.3 0.1 slice.21
  68.4 3.2 %fusion.15 = f32[1024,1024]{1,0:T(8,128)} fusion(bf16[1024,512]{1,0:T(8,128)(2,1)S(1)} %bitcast.126, bf16[64,8,8,128]{3,2,1,0:T(8,128)(2,1)S(1)} %bitcast.142), kind=kOutput, calls=%fused_computation.14 | convolution fusion | flops 1073741824 | bytes 6291456 | tf_op jit(solution)/shard_map/dot_general | solution.py:420
  71.6 0.0 reduce-scatter.2.cloned.1.call-update
  71.6 2.9 %fusion.1 = f32[64,8,8,128]{3,1,2,0:T(8,128)S(1)} fusion(bf16[2,8,4,32,1024]{4,3,2,1,0:T(8,128)(2,1)} %copy-done.1, bf16[2,8,4,32,512]{4,3,2,1,0:T(8,128)(2,1)S(1)} %get-tuple-element.11), kind=kOutput, calls=%fused_computation.3 | convolution fusion | flops 1074266112 | bytes 5242880 | tf_op jit(solution)/shard_map/dot_general | solution.py:14
  74.5 1.8 copy.45
  76.3 1.1 copy-done.2
  77.4 1.3 fusion.2
  78.7 2.5 %fusion.block = f32[512,1024]{1,0:T(8,128)S(1)} fusion(f32[512,1024,1,1]{1,0,3,2:T(8,128)S(1)} %fusion.2, bf16[2,8,4,32,1024]{4,3,2,1,0:T(8,128)(2,1)S(1)} %copy-done.2, bf16[2,8,4,32,512]{4,3,2,1,0:T(8,128)(2,1)} %copy-done), kind=kOutput, calls=%fused_computation.1 | convolution fusion | flops 1074790400 | bytes 7340032 | tf_op jit(solution)/shard_map/dot_general | solution.py:14
  81.2 0.5 copy.46
  81.7 0.1 slice.28
  81.8 0.1 copy.42
  81.9 136.6 %panel.1 = (f32[16,32,128]{2,1,0:T(8,128)S(1)}, f32[16,32,128]{2,1,0:T(8,128)S(1)}, f32[1,128]{1,0:T(1,128)S(1)}, f32[1,128]{1,0:T(1,128)S(1)}) custom-call(f32[512,1024]{1,0:T(8,128)S(1)} %fusion.block, f32[16,4,128]{2,1,0:T(4,128)S(1)} %select_bitcast_fusion.lead), custom_call_target="tpu_custom_call" | custom-call | flops 400000000 | bytes 4000000 | tf_op jit(solution)/shard_map/panel/pallas_call | solution.py:183
  218.6 0.2 copy.33
  218.7 0.2 copy.31
  219.1 1.9 subtract_bitcast_fusion
  221.0 1.8 copy.51
  222.8 0.5 slice_bitcast_fusion
  223.3 1.1 convert_bitcast_fusion
  224.4 0.8 copy.53
  (20 shorter events, 0.3 us)
Async XLA Ops:
  7.2 3.4 %copy-start.3 = (bf16[32,4096]{1,0:T(8,128)(2,1)S(1)}, bf16[32,4096]{1,0:T(8,128)(2,1)}, u32[]{:S(2)}) copy-start(bf16[32,4096]{1,0:T(8,128)(2,1)} %param.3) | copy-start | bytes 786436
  7.2 216.1 %reduce-scatter.2.cloned.1.call-start = ((), (), s32[]{:S(2)}) async-start(), calls=%async_computation.1 | async-start | bytes 4718592 | tf_op jit(solution)/shard_map/reduce_scatter | solution.py:419
  11.7 56.6 %copy-start.4 = (bf16[4,1,128,8,1,128]{5,3,4,2,1,0:T(8,128)(2,1)S(1)}, bf16[4,1,128,8,1,128]{5,3,4,2,1,0:T(8,128)(2,1)}, u32[]{:S(2)}) copy-start(bf16[4,1,128,8,1,128]{5,3,4,2,1,0:T(8,128)(2,1)} %param.5) | copy-start | bytes 3145732
  66.3 1.9 copy-start.1
  68.3 8.0 %copy-start = (bf16[2,8,4,32,512]{4,3,2,1,0:T(8,128)(2,1)}, bf16[2,8,4,32,512]{4,3,2,1,0:T(8,128)(2,1)S(1)}, u32[]{:S(2)}) copy-start(bf16[2,8,4,32,512]{4,3,2,1,0:T(8,128)(2,1)S(1)} %get-tuple-element.11) | copy-start | bytes 6291460
  74.5 2.9 %copy-start.2 = (bf16[2,8,4,32,1024]{4,3,2,1,0:T(8,128)(2,1)S(1)}, bf16[2,8,4,32,1024]{4,3,2,1,0:T(8,128)(2,1)}, u32[]{:S(2)}) copy-start(bf16[2,8,4,32,1024]{4,3,2,1,0:T(8,128)(2,1)} %copy-done.1) | copy-start | bytes 12582916
Sparse Core Ops, SparseCore 0:
  71.7 55.1 reduce-scatter.1

commit v3 on v2

--- a/solution.py
+++ b/solution.py
@@ -22,8 +22,9 @@
 
 def panel_kernel(
     sizes, block, lead, vecs, images, diagonal, offdiag,
-    panel, places, vector_now, folded, part, piece, gathered, full,
+    panel, places, vector_now, folded, part, full,
     lead_part, lead_piece, lead_all, col_send, col_recv, row_send, row_recv,
+    all_send, all_recv,
 ):
     row_count, col_count, row_tiles, col_tiles, tile = sizes
     row_id = lax.axis_index("row")
@@ -35,44 +36,60 @@
     def row_peer(distance):
         return (lax.rem(row_id + distance, row_count), col_id)
 
+    devices = row_count * col_count
+    flat_id = row_id * col_count + col_id
+
+    def any_peer(distance):
+        flat = lax.rem(flat_id + distance, devices)
+        return (lax.div(flat, col_count), lax.rem(flat, col_count))
+
     barrier = pltpu.get_barrier_semaphore()
-    for distance in range(1, col_count):
+    for distance in range(1, devices):
         pl.semaphore_signal(
-            barrier, inc=1, device_id=col_peer(distance), device_id_type=pl.DeviceIdType.MESH
-        )
-    for distance in range(1, row_count):
-        pl.semaphore_signal(
-            barrier, inc=1, device_id=row_peer(distance), device_id_type=pl.DeviceIdType.MESH
-        )
-    pl.semaphore_wait(barrier, row_count + col_count - 2)
-
-    def col_copies(source, target, slot):
+            barrier, inc=1, device_id=any_peer(distance), device_id_type=pl.DeviceIdType.MESH
+        )
+    pl.semaphore_wait(barrier, devices - 1)
+
+    def all_copies(place, slot):
+        return [
+            pltpu.make_async_remote_copy(
+                src_ref=place,
+                dst_ref=place,
+                send_sem=all_send.at[slot, distance],
+                recv_sem=all_recv.at[slot, distance],
+                device_id=any_peer(distance),
+                device_id_type=pl.DeviceIdType.MESH,
+            )
+            for distance in range(1, devices)
+        ]
+
+    def col_copies(source, target):
         return [
             pltpu.make_async_remote_copy(
                 src_ref=source,
                 dst_ref=target,
-                send_sem=col_send.at[slot, distance],
-                recv_sem=col_recv.at[slot, distance],
+                send_sem=col_send.at[distance],
+                recv_sem=col_recv.at[distance],
                 device_id=col_peer(distance),
                 device_id_type=pl.DeviceIdType.MESH,
             )
             for distance in range(1, col_count)
         ]
 
-    def row_copies(source, target, slot):
+    def row_copies(source, target):
         return [
             pltpu.make_async_remote_copy(
                 src_ref=source,
                 dst_ref=target,
-                send_sem=row_send.at[slot, distance],
-                recv_sem=row_recv.at[slot, distance],
+                send_sem=row_send.at[distance],
+                recv_sem=row_recv.at[distance],
                 device_id=row_peer(distance),
                 device_id_type=pl.DeviceIdType.MESH,
             )
             for distance in range(1, row_count)
         ]
 
-    copies = col_copies(lead, lead_part.at[col_id], 2)
+    copies = col_copies(lead, lead_part.at[col_id])
     for copy in copies:
         copy.start()
     lead_part[pl.ds(col_id, 1)] = lead[...][None]
@@ -92,7 +109,7 @@
     for source in range(1, col_count):
         summed = summed + lead_part[source]
     lead_piece[...] = summed
-    copies = row_copies(lead_piece, lead_all.at[row_id], 2)
+    copies = row_copies(lead_piece, lead_all.at[row_id])
     for copy in copies:
         copy.start()
     lead_all[pl.ds(row_id, 1)] = summed[None]
@@ -145,8 +162,8 @@
             preferred_element_type=jnp.float32,
         )
         for t in range(row_tiles):
-            part[step, col_id, t : t + 1, :] = sums[0:1, t * tile : (t + 1) * tile]
-        sent = col_copies(part.at[step, col_id], part.at[step, col_id], slot)
+            part[step, row_id, col_id, t : t + 1, :] = sums[0:1, t * tile : (t + 1) * tile]
+        sent = all_copies(part.at[step, row_id, col_id], slot)
         for copy in sent:
             copy.start()
         onto_w = [total(images[k] * vector) for k in range(PB - 1)]
@@ -159,17 +176,11 @@
         offdiag[...] = jnp.where(lane == step, beta, offdiag[...])
         for copy in sent:
             copy.wait()
-        image = part[step, 0]
-        for source in range(1, col_count):
-            image = image + part[step, source]
-        gathered[step, row_id] = image
-        sent = row_copies(gathered.at[step, row_id], gathered.at[step, row_id], slot)
-        for copy in sent:
-            copy.start()
-        for copy in sent:
-            copy.wait()
         for owner in range(row_count):
-            full[owner * row_tiles : (owner + 1) * row_tiles, :] = gathered[step, owner]
+            piece = part[step, owner, 0]
+            for source in range(1, col_count):
+                piece = piece + part[step, owner, source]
+            full[owner * row_tiles : (owner + 1) * row_tiles, :] = piece
         image = tau * (full[...] - fix)
         image = image - 0.5 * tau * total(image * vector) * vector
         images[pl.ds(step, 1)] = image[None]
@@ -195,17 +206,17 @@
             pltpu.VMEM((all_tiles, tile), jnp.int32),
             pltpu.VMEM((all_tiles, tile), f32),
             pltpu.VMEM((row_tiles * tile, tile), f32),
-            pltpu.VMEM((PB, col_count, row_tiles, tile), f32),
-            pltpu.VMEM((row_tiles, tile), f32),
-            pltpu.VMEM((PB, row_count, row_tiles, tile), f32),
+            pltpu.VMEM((PB, row_count, col_count, row_tiles, tile), f32),
             pltpu.VMEM((all_tiles, tile), f32),
             pltpu.VMEM((col_count, PB, row_tiles, tile), f32),
             pltpu.VMEM((PB, row_tiles, tile), f32),
             pltpu.VMEM((row_count, PB, row_tiles, tile), f32),
-            pltpu.SemaphoreType.DMA((3, col_count)),
-            pltpu.SemaphoreType.DMA((3, col_count)),
-            pltpu.SemaphoreType.DMA((3, row_count)),
-            pltpu.SemaphoreType.DMA((3, row_count)),
+            pltpu.SemaphoreType.DMA((col_count,)),
+            pltpu.SemaphoreType.DMA((col_count,)),
+            pltpu.SemaphoreType.DMA((row_count,)),
+            pltpu.SemaphoreType.DMA((row_count,)),
+            pltpu.SemaphoreType.DMA((2, row_count * col_count)),
+            pltpu.SemaphoreType.DMA((2, row_count * col_count)),
         ],
         compiler_params=pltpu.CompilerParams(
             collective_id=0, has_side_effects=True, vmem_limit_bytes=24 * 1024 * 1024

time: 232 us -> 207 us (0.89)
  Pallas kernels: 191 us -> 166 us
    pallas_call x1, Pallas kernels: 137 us -> 111 us  [reduce_panel(): pl.pallas_call(functools.partial(panel_kernel, sizes), out_shape=(jax.Sha...]
  transfers between devices with their start and end apart: 1 -> 1, of which waited for: 0 -> 0; matrix products, arithmetic and copies ran while one was open for 6% -> 7% of each run, Pallas kernels for 59% -> 54%
where the time goes in v3:
time: 207 us
  Pallas kernels  166 us (80%)
  between operations  14.3 us (7%)
  local copies, waits for them, and re-layouts  13.2 us (6%)
  matrix products  11.7 us (6%)
    pallas_call x1, Pallas kernels, reduce_panel(): pl.pallas_call(functools.partial(panel_kernel, sizes), out_shape=(jax.Sha...  111 us
    pallas_call x1, Pallas kernels, spread(): pl.pallas_call(functools.partial(spread_kernel, row_count, col_count), ou...  54.6 us
    unnamed x21, local copies, waits for them, and re-layouts  9.07 us
    dot_general x3, matrix products, inner(): lax.dot_general(left, right, (((0,), (0,)), ((), ())), preferred_element_...  6.62 us
  transfers between devices with their start and end apart: 1, of which 0 were waited for; matrix products, arithmetic and copies ran while one was open for 7% of the time, Pallas kernels for 54%

profile of v3, /device:TPU:0, one launch (start us, length us, event | category | flops | bytes accessed | tf_op | source)
XLA Modules:
  0.0 206.6 jit_solution(6574564438319515929)
XLA Ops:
  7.2 0.0 copy-start.3
  7.2 0.0 reduce-scatter.2.cloned.1.call-start
  7.2 1.2 stack.19
  8.4 1.0 copy.44
  9.4 0.1 copy.27
  9.5 1.1 stack.18
  10.7 0.1 copy.26
  10.8 0.3 maximum_bitcast_fusion
  11.1 0.2 reshape.88.rows_in
  11.4 0.1 maximum_bitcast_fusion.1
  11.5 0.2 reshape.89.cols_in
  11.7 54.6 %spread.1 = (bf16[2,8,4,32,512]{4,3,2,1,0:T(8,128)(2,1)S(1)}, bf16[2,8,4,32,1024]{4,3,2,1,0:T(8,128)(2,1)S(1)}) custom-call(bf16[8,2,32,512]{3,2,1,0:T(8,128)(2,1)S(1)} %reshape.88.rows_in, bf16[4,2,32,1024]{3,2,1,0:T(8,128)(2,1)S(1)} %reshape.89.cols_in), custom_call_target="tpu_custom_call" | custom-call | flops 100000000 | bytes 8000000 | tf_op jit(solution)/shard_map/spread/pallas_call | solution.py:349
  66.3 1.9 copy-done.1
  68.3 0.1 slice.21
  68.4 3.2 %fusion.15 = f32[1024,1024]{1,0:T(8,128)} fusion(bf16[1024,512]{1,0:T(8,128)(2,1)S(1)} %bitcast.126, bf16[64,8,8,128]{3,2,1,0:T(8,128)(2,1)S(1)} %bitcast.142), kind=kOutput, calls=%fused_computation.14 | convolution fusion | flops 1073741824 | bytes 6291456 | tf_op jit(solution)/shard_map/dot_general | solution.py:431
  71.6 0.0 reduce-scatter.2.cloned.1.call-update
  71.6 2.9 %fusion.1 = f32[64,8,8,128]{3,1,2,0:T(8,128)S(1)} fusion(bf16[2,8,4,32,1024]{4,3,2,1,0:T(8,128)(2,1)} %copy-done.1, bf16[2,8,4,32,512]{4,3,2,1,0:T(8,128)(2,1)S(1)} %get-tuple-element.11), kind=kOutput, calls=%fused_computation.3 | convolution fusion | flops 1074266112 | bytes 5242880 | tf_op jit(solution)/shard_map/dot_general | solution.py:14
  74.5 1.8 copy.45
  76.3 1.1 copy-done.2
  77.4 1.3 fusion.2
  78.7 2.5 %fusion.block = f32[512,1024]{1,0:T(8,128)S(1)} fusion(f32[512,1024,1,1]{1,0,3,2:T(8,128)S(1)} %fusion.2, bf16[2,8,4,32,1024]{4,3,2,1,0:T(8,128)(2,1)S(1)} %copy-done.2, bf16[2,8,4,32,512]{4,3,2,1,0:T(8,128)(2,1)} %copy-done), kind=kOutput, calls=%fused_computation.1 | convolution fusion | flops 1074790400 | bytes 7340032 | tf_op jit(solution)/shard_map/dot_general | solution.py:14
  81.2 0.5 copy.46
  81.7 0.1 slice.28
  81.8 0.1 copy.42
  81.9 111.2 %panel.1 = (f32[16,32,128]{2,1,0:T(8,128)S(1)}, f32[16,32,128]{2,1,0:T(8,128)S(1)}, f32[1,128]{1,0:T(1,128)S(1)}, f32[1,128]{1,0:T(1,128)S(1)}) custom-call(f32[512,1024]{1,0:T(8,128)S(1)} %fusion.block, f32[16,4,128]{2,1,0:T(4,128)S(1)} %select_bitcast_fusion.lead), custom_call_target="tpu_custom_call" | custom-call | flops 400000000 | bytes 4000000 | tf_op jit(solution)/shard_map/panel/pallas_call | solution.py:194
  193.2 0.2 copy.33
  193.3 0.2 copy.31
  193.7 1.9 subtract_bitcast_fusion
  195.6 1.8 copy.51
  197.4 0.5 slice_bitcast_fusion
  197.9 1.1 convert_bitcast_fusion
  199.0 0.8 copy.53
  (20 shorter events, 0.3 us)
Async XLA Ops:
  7.2 3.4 %copy-start.3 = (bf16[32,4096]{1,0:T(8,128)(2,1)S(1)}, bf16[32,4096]{1,0:T(8,128)(2,1)}, u32[]{:S(2)}) copy-start(bf16[32,4096]{1,0:T(8,128)(2,1)} %param.3) | copy-start | bytes 786436
  7.2 190.7 %reduce-scatter.2.cloned.1.call-start = ((), (), s32[]{:S(2)}) async-start(), calls=%async_computation.1 | async-start | bytes 4718592 | tf_op jit(solution)/shard_map/reduce_scatter | solution.py:430
  11.7 56.6 %copy-start.4 = (bf16[4,1,128,8,1,128]{5,3,4,2,1,0:T(8,128)(2,1)S(1)}, bf16[4,1,128,8,1,128]{5,3,4,2,1,0:T(8,128)(2,1)}, u32[]{:S(2)}) copy-start(bf16[4,1,128,8,1,128]{5,3,4,2,1,0:T(8,128)(2,1)} %param.5) | copy-start | bytes 3145732
  66.3 1.9 copy-start.1
  68.3 8.0 %copy-start = (bf16[2,8,4,32,512]{4,3,2,1,0:T(8,128)(2,1)}, bf16[2,8,4,32,512]{4,3,2,1,0:T(8,128)(2,1)S(1)}, u32[]{:S(2)}) copy-start(bf16[2,8,4,32,512]{4,3,2,1,0:T(8,128)(2,1)S(1)} %get-tuple-element.11) | copy-start | bytes 6291460
  74.5 2.9 %copy-start.2 = (bf16[2,8,4,32,1024]{4,3,2,1,0:T(8,128)(2,1)S(1)}, bf16[2,8,4,32,1024]{4,3,2,1,0:T(8,128)(2,1)}, u32[]{:S(2)}) copy-start(bf16[2,8,4,32,1024]{4,3,2,1,0:T(8,128)(2,1)} %copy-done.1) | copy-start | bytes 12582916
Sparse Core Ops, SparseCore 0:
  71.7 58.6 reduce-scatter.1
